TPU v7x, 32 devices: a whole 2x2x4 slice. The times are simulated.
32 devices in a mesh: tm: 2 (over y), row: 4 (over z), col: 4 (over x, core).
Axes of the slice: x: 2, y: 2, z: 4, core: 2. Of those that a mesh axis runs over, the one named last changes fastest.
Arguments:
- returns: bfloat16 [272, 16384], P('tm', ('row', 'col')), may hold values from -60 to 60
- window: int32 [1], replicated, may hold values from 200 to 256
- out_days: int32 [4], replicated, may hold values from 255 to 271
Outputs:
- correlation: bfloat16 [4, 16384, 16384], P(None, 'row', ('col', 'tm'))
Inputs may be any that keep to these rules, and one draw needn't show every extreme that they name: One window length for all days. `out_days`: days may repeat.
All inputs are finite; a program needn't handle non-finite values.
Results may differ from a plain program's by a relative error of at most 0.001.
Values may be sent and summed in bfloat16 or wider, within the bound.
A program may use at most 128 MiB of HBM per device.

v0:
```python
import functools

import jax
import jax.numpy as jnp
from jax import lax
from jax.experimental import pallas as pl
from jax.experimental.pallas import tpu as pltpu
from jax.sharding import PartitionSpec as P

MESH = pl.DeviceIdType.MESH


def gather_kernel(T, R, C, x_ref, row_ref, col_ref, line, line_send, line_recv,
                  row_send, row_recv, twin_send, twin_recv, col_send, col_recv, local_sem):
    t, r, c = lax.axis_index("tm"), lax.axis_index("row"), lax.axis_index("col")
    n = R // T
    core = lax.rem(c, 2)
    twin = c + 1 - 2 * core
    chips = C // 2

    def to(tt, rr, cc):
        return {"tm": tt, "row": rr, "col": cc}

    barrier = pltpu.get_barrier_semaphore()
    for d in range(1, T * C):
        flat = lax.rem(t * C + c + d, T * C)
        pl.semaphore_signal(barrier, inc=1, device_id=to(flat // C, r, lax.rem(flat, C)), device_id_type=MESH)

    @pl.when(r > 0)
    def _():
        pl.semaphore_signal(barrier, inc=1, device_id=to(t, r - 1, c), device_id_type=MESH)

    @pl.when(r < R - 1)
    def _():
        pl.semaphore_signal(barrier, inc=1, device_id=to(t, r + 1, c), device_id_type=MESH)

    inner = jnp.logical_and(r > 0, r < R - 1)
    pl.semaphore_wait(barrier, T * C + inner.astype(jnp.int32) if R > 1 else T * C - 1)

    def rdma(src, dst, send, recv, device):
        return pltpu.make_async_remote_copy(src_ref=src, dst_ref=dst, send_sem=send, recv_sem=recv,
                                            device_id=device, device_id_type=MESH)

    def line_copy(src, q, up):
        return rdma(src, line.at[q], line_send.at[int(up), q], line_recv.at[q],
                    to(t, r + (1 if up else -1), c))

    def send_line(src, q, up):
        ok = (r < R - 1) if up else (r > 0)

        @pl.when(ok)
        def _():
            line_copy(src, q, up).start()

    def col_place(q):
        piece = q * C + c
        group = piece // n
        return lax.rem(group, T), group // T, lax.rem(piece, n)

    def col_copy(src, q):
        tt, cc, j = col_place(q)
        return rdma(src, col_ref.at[t, j], col_send.at[q], col_recv.at[t, j], to(tt, r, cc))

    def send_col(src, q):
        tt, cc, j = col_place(q)
        mine = jnp.logical_and(tt == t, cc == c)

        @pl.when(mine)
        def _():
            pltpu.make_async_copy(src, col_ref.at[t, j], col_recv.at[t, j]).start()

        @pl.when(jnp.logical_not(mine))
        def _():
            col_copy(src, q).start()

    own_out = pltpu.make_async_copy(x_ref, row_ref.at[t, c], local_sem)
    send_line(x_ref, r, True)
    send_line(x_ref, r, False)

    def row_copy(d):
        flat = lax.rem(t * chips + c // 2 + d, T * chips)
        return rdma(x_ref, row_ref.at[t, c], row_send.at[d], row_recv.at[d],
                    to(flat // chips, r, 2 * lax.rem(flat, chips) + core))

    for d in range(1, T * chips):
        row_copy(d).start()
    rdma(x_ref, row_ref.at[t, c], twin_send.at[0], twin_recv.at[0], to(t, r, twin)).start()
    own_out.start()
    send_col(x_ref, r)

    def row_arrived(d):
        flat = lax.rem(t * chips + c // 2 - d + T * chips, T * chips)
        slot = row_ref.at[flat // chips, 2 * lax.rem(flat, chips) + core]
        rdma(slot, slot, row_send.at[d], row_recv.at[d], to(t, r, twin)).wait_recv()
        rdma(slot, slot, twin_send.at[d], twin_recv.at[d], to(t, r, twin)).start()

    def line_arrived(dist):
        for up in (True, False):
            q = r - dist if up else r + dist
            ok = (q >= 0) if up else (q < R)

            @pl.when(ok)
            def _():
                line_copy(line.at[q], q, up).wait_recv()
                send_line(line.at[q], q, up)
                send_col(line.at[q], q)

    for dist in range(1, R):
        line_arrived(dist)
        if dist == 1:
            for d in range(1, T * chips):
                row_arrived(d)

    own_out.wait()
    for d in range(1, T * chips):
        row_copy(d).wait_send()
    for d in range(T * chips):
        flat = lax.rem(t * chips + c // 2 - d + T * chips, T * chips)
        mine = row_ref.at[flat // chips, 2 * lax.rem(flat, chips) + core]
        theirs = row_ref.at[flat // chips, 2 * lax.rem(flat, chips) + 1 - core]
        rdma(mine, mine, twin_send.at[d], twin_recv.at[d], to(t, r, twin)).wait_send()
        rdma(theirs, theirs, twin_send.at[d], twin_recv.at[d], to(t, r, twin)).wait_recv()
    for tt in range(T):
        for j in range(n):
            slot = col_ref.at[tt, j]
            pltpu.make_async_copy(slot, slot, col_recv.at[tt, j]).wait()
    for q in range(R):
        tt, cc, j = col_place(q)

        @pl.when(jnp.logical_not(jnp.logical_and(tt == t, cc == c)))
        def _():
            col_copy(x_ref, q).wait_send()

        @pl.when(jnp.logical_and(q <= r, r < R - 1))
        def _():
            line_copy(x_ref, q, True).wait_send()

        @pl.when(jnp.logical_and(q >= r, r > 0))
        def _():
            line_copy(x_ref, q, False).wait_send()


def gather(returns, T, R, C):
    days, width = returns.shape
    n = R // T
    dma = pltpu.SemaphoreType.DMA
    chips = T * C // 2
    return pl.pallas_call(
        functools.partial(gather_kernel, T, R, C),
        out_shape=(
            jax.ShapeDtypeStruct((T, C, days, width), returns.dtype),
            jax.ShapeDtypeStruct((T, n, days, width), returns.dtype),
        ),
        in_specs=[pl.BlockSpec(memory_space=pltpu.VMEM)],
        out_specs=(pl.BlockSpec(memory_space=pl.ANY), pl.BlockSpec(memory_space=pl.ANY)),
        scratch_shapes=[
            pltpu.VMEM((R, days, width), returns.dtype),
            dma((2, R)), dma((R,)),
            dma((chips,)), dma((chips,)),
            dma((chips,)), dma((chips,)),
            dma((R,)), dma((T, n)), dma,
        ],
        compiler_params=pltpu.CompilerParams(collective_id=0, has_side_effects=True),
    )(returns)


def corr_kernel(tile, depth, window_ref, out_ref_days, row_ref, col_ref, o_ref,
                rows_t, cols, col_a, col_m):
    i, k = pl.program_id(0), pl.program_id(1)
    K = out_ref_days.shape[0]
    T, n, half_days, width = col_ref.shape
    days = T * half_days
    extra = days - depth
    w = window_ref[0]
    wide = w.astype(jnp.float32)
    recip = 1.0 / wide

    def slot_mask(shape, dim, last):
        s = lax.broadcasted_iota(jnp.int32, shape, dim)
        day = jnp.where(s + depth <= last, s + depth, s)
        return (day <= last) & (day > last - w)

    def joined(ref, at):
        return jnp.concatenate([ref[tt, at] for tt in range(T)], axis=0)

    @pl.when((i == 0) & (k == 0))
    def _():
        for j in range(n):
            x = joined(col_ref, j)
            at = pl.ds(j * width, width)
            for kk in range(K):
                last = out_ref_days[kk]
                slot = lax.broadcasted_iota(jnp.int32, (extra, width), 0)
                head = jnp.where(slot + depth <= last, x[depth:].astype(jnp.float32),
                                 x[:extra].astype(jnp.float32)).astype(x.dtype)
                cols[kk, :extra, at] = head
                cols[kk, extra:, at] = x[extra:depth]
                f = jnp.where(slot_mask((depth, width), 0, last),
                              cols[kk, :, at].astype(jnp.float32), 0.0)
                first = jnp.sum(f, axis=0, keepdims=True)
                second = jnp.sum(f * f, axis=0, keepdims=True)
                scale = lax.rsqrt((second - first * first / wide) / wide + 1e-06)
                col_a[kk, :, at] = scale * recip
                col_m[kk, :, at] = first * recip * (scale * recip)

    per_piece = width // tile if width >= tile else 1

    @pl.when(k == 0)
    def _():
        piece = i // per_piece
        at = pl.ds(pl.multiple_of(lax.rem(i, per_piece) * tile, 128), tile)
        x = jnp.concatenate([row_ref[tt, piece, :, at] for tt in range(T)], axis=0)
        rows_t[:, :depth] = x[:depth].T
        tail = jnp.concatenate([x[depth:], jnp.zeros((128 - extra, tile), x.dtype)], axis=0)
        rows_t[:, depth:] = tail.T

    last = out_ref_days[k]
    lane = lax.broadcasted_iota(jnp.int32, (tile, 128), 1)
    use = (lane < extra) & (lane + depth <= last)
    head = jnp.where(use, rows_t[:, depth:].astype(jnp.float32), rows_t[:, :128].astype(jnp.float32))
    f = jnp.concatenate([head, rows_t[:, 128:depth].astype(jnp.float32)], axis=1)
    f = jnp.where(slot_mask((tile, depth), 1, last), f, 0.0)
    lhs = f.astype(jnp.bfloat16)
    first = jnp.dot(lhs, jnp.ones((depth, 128), lhs.dtype), preferred_element_type=jnp.float32)
    second = jnp.sum(f * f, axis=1, keepdims=True)
    scale = lax.rsqrt((second - first * first / wide) / wide + 1e-06)
    m = first * scale
    N = cols.shape[2]
    step = 256 if N % 256 == 0 else 128
    scale = jnp.concatenate([scale] * (step // 128), axis=1)
    m = jnp.concatenate([m] * (step // 128), axis=1)
    for b in range(0, N, step):
        g = jnp.dot(lhs, cols[k, :, b:b + step], preferred_element_type=jnp.float32)
        o = (g * scale) * col_a[k, :, b:b + step] - m * col_m[k, :, b:b + step]
        o_ref[0, :, b:b + step] = o.astype(o_ref.dtype)


def correlate(window, out_days, rows, cols):
    T, C, half_days, width = rows.shape
    n = cols.shape[1]
    K = out_days.shape[0]
    M, N = C * width, n * width
    depth = 256
    tile = min(512, width)
    grid_spec = pltpu.PrefetchScalarGridSpec(
        num_scalar_prefetch=2,
        grid=(M // tile, K),
        in_specs=[
            pl.BlockSpec(rows.shape, lambda i, k, *_: (0, 0, 0, 0)),
            pl.BlockSpec(cols.shape, lambda i, k, *_: (0, 0, 0, 0)),
        ],
        out_specs=pl.BlockSpec((1, tile, N), lambda i, k, *_: (k, i, 0)),
        scratch_shapes=[
            pltpu.VMEM((tile, depth + 128), jnp.bfloat16),
            pltpu.VMEM((K, depth, N), jnp.bfloat16),
            pltpu.VMEM((K, 1, N), jnp.float32),
            pltpu.VMEM((K, 1, N), jnp.float32),
        ],
    )
    return pl.pallas_call(
        functools.partial(corr_kernel, tile, depth),
        out_shape=jax.ShapeDtypeStruct((K, M, N), jnp.bfloat16),
        grid_spec=grid_spec,
        compiler_params=pltpu.CompilerParams(
            dimension_semantics=("arbitrary", "arbitrary"), vmem_limit_bytes=60 * 2**20),
    )(window, out_days, rows, cols)


def on_device(returns, window, out_days):
    T, R, C = lax.axis_size("tm"), lax.axis_size("row"), lax.axis_size("col")
    rows, cols = gather(returns, T, R, C)
    return correlate(window, out_days, rows, cols)


def solution(mesh):
    return jax.shard_map(
        on_device,
        mesh=mesh,
        in_specs=(P("tm", ("row", "col")), P(), P()),
        out_specs=P(None, "row", ("col", "tm")),
        check_vma=False,
    )
```

profile of v0, /device:TPU:0, one launch (start us, length us, event | category | flops | bytes accessed | tf_op | source)
XLA Modules:
  0.0 79.3 jit_solution(12871809425544965095)
XLA Ops:
  0.7 34.1 %shard_map.37 = (bf16[2,4,136,1024]{3,2,1,0:T(8,128)(2,1)}, bf16[2,2,136,1024]{3,2,1,0:T(8,128)(2,1)}) custom-call(bf16[136,1024]{1,0:T(8,128)(2,1)} %x_ref.1), custom_call_target="tpu_custom_call" | custom-call | tf_op jit(solution)/shard_map/pallas_call | solution.py:148
  34.7 44.6 %shard_map.38 = bf16[4,4096,2048]{2,1,0:T(8,128)(2,1)} custom-call(s32[1]{0:T(128)S(6)} %copy.4.window_ref, s32[4]{0:T(128)} %out_ref_days.1, bf16[2,4,136,1024]{3,2,1,0:T(8,128)(2,1)} %get-tuple-element.7.row_ref, bf16[2,2,136,1024]{3,2,1,0:T(8,128)(2,1)} %get-tuple-element.8.col_ref), custom_call_target="tpu_custom_call" | custom-call | tf_op jit(solution)/shard_map/pallas_call | solution.py:260
where the time goes:
time: 79.5 us; the launch traced here: 79.3 us
  Pallas kernels  78.7 us (99%)
    pallas_call x1, Pallas kernels, correlate(): pl.pallas_call(functools.partial(corr_kernel, tile, depth), out_shape=jax...  44.6 us
    pallas_call x1, Pallas kernels, gather(): pl.pallas_call(functools.partial(gather_kernel, T, R, C), out_shape=(jax....  34.1 us

commit v1 on v0

v1 whole, which is shorter than its diff:
```python
import functools

import jax
import jax.numpy as jnp
from jax import lax
from jax.experimental import pallas as pl
from jax.experimental.pallas import tpu as pltpu
from jax.sharding import PartitionSpec as P

MESH = pl.DeviceIdType.MESH


def gather_kernel(T, R, C, S, x_ref, rows_ref, cols_ref, line, line_send, line_recv,
                  row_send, row_recv, twin_send, relay_send, col_send, col_recv, local_sem):
    t, r, c = lax.axis_index("tm"), lax.axis_index("row"), lax.axis_index("col")
    half, width = x_ref.shape
    sub = width // S
    n = R // T
    core = lax.rem(c, 2)
    twin = c + 1 - 2 * core
    chips = C // 2
    chip = c // 2

    def to(tt, rr, cc):
        return {"tm": tt, "row": rr, "col": cc}

    barrier = pltpu.get_barrier_semaphore()
    for d in range(1, T * C):
        flat = lax.rem(t * C + c + d, T * C)
        pl.semaphore_signal(barrier, inc=1, device_id=to(flat // C, r, lax.rem(flat, C)), device_id_type=MESH)

    @pl.when(r > 0)
    def _():
        pl.semaphore_signal(barrier, inc=1, device_id=to(t, r - 1, c), device_id_type=MESH)

    @pl.when(r < R - 1)
    def _():
        pl.semaphore_signal(barrier, inc=1, device_id=to(t, r + 1, c), device_id_type=MESH)

    inner = jnp.logical_and(r > 0, r < R - 1)
    pl.semaphore_wait(barrier, T * C + inner.astype(jnp.int32) if R > 1 else T * C - 1)

    def rdma(src, dst, send, recv, device):
        return pltpu.make_async_remote_copy(src_ref=src, dst_ref=dst, send_sem=send, recv_sem=recv,
                                            device_id=device, device_id_type=MESH)

    def part(s):
        return x_ref.at[:, pl.ds(s * sub, sub)]

    def row_slot(tt, cc, s):
        return rows_ref.at[pl.ds(pl.multiple_of(tt * half, 8), half),
                           pl.ds(pl.multiple_of(cc * width + s * sub, sub), sub)]

    def col_slot(tt, j, s):
        return cols_ref.at[pl.ds(pl.multiple_of(tt * half, 8), half),
                           pl.ds(pl.multiple_of(j * width + s * sub, sub), sub)]

    def line_copy(src, q, s, up):
        return rdma(src, line.at[q, s], line_send.at[int(up), q, s], line_recv.at[q, s],
                    to(t, r + (1 if up else -1), c))

    def send_line(src, q, s, up):
        ok = (r < R - 1) if up else (r > 0)

        @pl.when(ok)
        def _():
            line_copy(src, q, s, up).start()

    def col_place(q):
        piece = q * C + c
        group = piece // n
        return lax.rem(group, T), group // T, lax.rem(piece, n)

    def col_copy(src, q, s):
        tt, cc, j = col_place(q)
        return rdma(src, col_slot(t, j, s), col_send.at[q, s], col_recv.at[t, j, s], to(tt, r, cc))

    def send_col(src, q, s):
        tt, cc, j = col_place(q)
        mine = jnp.logical_and(tt == t, cc == c)

        @pl.when(mine)
        def _():
            pltpu.make_async_copy(src, col_slot(t, j, s), col_recv.at[t, j, s]).start()

        @pl.when(jnp.logical_not(mine))
        def _():
            col_copy(src, q, s).start()

    near = [(dt, dx) for dt in range(T) for dx in range(chips) if dt or dx]
    far = []

    def at_chip(dt, dx):
        return lax.rem(t + dt + T, T), 2 * lax.rem(chip + dx + chips, chips) + core

    def own_copy(i, s):
        tt, cc = at_chip(*near[i])
        return rdma(part(s), row_slot(t, c, s), row_send.at[i, s], row_recv.at[t, c, s], to(tt, r, cc))

    def own_twin(s):
        return rdma(part(s), row_slot(t, c, s), row_send.at[len(near), s], row_recv.at[t, c, s], to(t, r, twin))

    def twin_copy(dt, dx, s):
        tt, cc = at_chip(-dt, -dx)
        slot = row_slot(tt, cc, s)
        return rdma(slot, slot, twin_send.at[dt, dx, s], row_recv.at[tt, cc, s], to(t, r, twin))

    def relays(dt, dx):
        if dt == 0:
            return core == 0, [(d, 0) for d in range(1, T)]
        return core == 1, [(0, d) for d in range(1, chips)]

    def relay_copy(dt, dx, hop, s):
        tt, cc = at_chip(-dt, -dx)
        slot = row_slot(tt, cc, s)
        ht, hc = at_chip(*hop)
        return rdma(slot, slot, relay_send.at[dt, dx, max(hop) - 1, s], row_recv.at[tt, cc, s], to(ht, r, hc))

    def row_arrived(dt, dx, s):
        twin_copy(dt, dx, s).wait_recv()
        if False:
            ok, hops = relays(dt, dx)

            @pl.when(ok)
            def _():
                for hop in hops:
                    relay_copy(dt, dx, hop, s).start()
        twin_copy(dt, dx, s).start()

    def line_arrived(dist, s):
        for up in (True, False):
            q = r - dist if up else r + dist
            ok = (q >= 0) if up else (q < R)

            @pl.when(ok)
            def _():
                line_copy(line.at[q, s], q, s, up).wait_recv()
                send_line(line.at[q, s], q, s, up)
                send_col(line.at[q, s], q, s)

    own_out = pltpu.make_async_copy(x_ref, rows_ref.at[pl.ds(pl.multiple_of(t * half, 8), half),
                                                       pl.ds(pl.multiple_of(c * width, width), width)], local_sem)
    for s in range(S):
        send_line(part(s), r, s, True)
        send_line(part(s), r, s, False)
    for s in range(S):
        for i in range(len(near)):
            own_copy(i, s).start()
    for s in range(S):
        own_twin(s).start()
        send_col(part(s), r, s)
    own_out.start()

    for dist in range(1, R):
        for s in range(S):
            line_arrived(dist, s)
            if dist == min(2, R - 1) and s == S - 1:
                for s2 in range(S):
                    for dt, dx in near:
                        row_arrived(dt, dx, s2)
            if dist == min(2, R - 1):
                for dt, dx in far:
                    row_arrived(dt, dx, s)

    own_out.wait()
    for s in range(S):
        for i in range(len(near)):
            own_copy(i, s).wait_send()
        own_twin(s).wait_send()
        own_twin_slot = row_slot(t, twin, s)
        rdma(own_twin_slot, own_twin_slot, row_send.at[len(near), s], row_recv.at[t, twin, s], to(t, r, twin)).wait_recv()
        for dt, dx in near + far:
            twin_copy(dt, dx, s).wait_send()
            tt, cc = at_chip(-dt, -dx)
            theirs = row_slot(tt, cc + 1 - 2 * core, s)
            rdma(theirs, theirs, twin_send.at[dt, dx, s], row_recv.at[tt, cc + 1 - 2 * core, s], to(t, r, twin)).wait_recv()
    for s in range(S):
        for tt in range(T):
            for j in range(n):
                slot = col_slot(tt, j, s)
                pltpu.make_async_copy(slot, slot, col_recv.at[tt, j, s]).wait()
        for q in range(R):
            tt, cc, j = col_place(q)

            @pl.when(jnp.logical_not(jnp.logical_and(tt == t, cc == c)))
            def _():
                col_copy(part(s), q, s).wait_send()

            @pl.when(jnp.logical_and(q <= r, r < R - 1))
            def _():
                line_copy(part(s), q, s, True).wait_send()

            @pl.when(jnp.logical_and(q >= r, r > 0))
            def _():
                line_copy(part(s), q, s, False).wait_send()


def gather(returns, T, R, C, S=2):
    half, width = returns.shape
    n = R // T
    S = S if width % (128 * S) == 0 else 1
    sub = width // S
    dma = pltpu.SemaphoreType.DMA
    chips = C // 2
    near = T * chips - 1
    dt = returns.dtype
    return pl.pallas_call(
        functools.partial(gather_kernel, T, R, C, S),
        out_shape=(
            jax.ShapeDtypeStruct((T * half, C * width), dt),
            jax.ShapeDtypeStruct((T * half, n * width), dt),
        ),
        in_specs=[pl.BlockSpec(memory_space=pltpu.VMEM)],
        out_specs=(pl.BlockSpec(memory_space=pl.ANY), pl.BlockSpec(memory_space=pl.ANY)),
        scratch_shapes=[
            pltpu.VMEM((R, S, half, sub), dt),
            dma((2, R, S)), dma((R, S)),
            dma((near + 1, S)), dma((T, C, S)), dma((T, chips, S)), dma((T, chips, max(T, chips), S)),
            dma((R, S)), dma((T, n, S)), dma,
        ],
        compiler_params=pltpu.CompilerParams(collective_id=0, has_side_effects=True),
    )(returns)


DEPTH = 256
FOLD = 6
BF = jnp.bfloat16
F32 = jnp.float32


def split3(v):
    hi = v.astype(BF).astype(F32)
    mid = (v - hi).astype(BF).astype(F32)
    return hi, mid, v - hi - mid


def indicator(cond):
    return jnp.where(cond, 1.0, 0.0).astype(BF)


def wide_mask(m, width):
    return jnp.concatenate([m] * (width // 128), axis=1)


def corr_kernel(tile, chunk, window_ref, days_ref, row_ref, col_ref, out_ref,
                row_head, row_rest, col_head, col_a, col_m, row_stat, obuf, sems):
    K = days_ref.shape[0]
    days, M = row_ref.shape
    N = col_ref.shape[1]
    extra = days - DEPTH
    w = window_ref[0]
    wide = w.astype(F32)
    recip = 1.0 / wide
    fold = w <= DEPTH - FOLD

    kk = lax.broadcasted_iota(jnp.int32, (16, days), 0)
    day = lax.broadcasted_iota(jnp.int32, (16, days), 1)
    lasts = jnp.full((16, days), -1, jnp.int32)
    for k in range(K):
        lasts = jnp.where(kk == k, days_ref[k], lasts)
    inside = indicator((day <= lasts) & (day > lasts - w))

    slot = lax.broadcasted_iota(jnp.int32, (16, 128), 0)

    def stats(x):
        xf = x.astype(F32)
        sq = xf * xf
        hi = sq.astype(BF)
        lo = (sq - hi.astype(F32)).astype(BF)
        dot = functools.partial(jnp.dot, preferred_element_type=F32)
        first = dot(inside, x)
        second = dot(inside, hi) + dot(inside, lo)
        scale = lax.rsqrt((second - first * first / wide) / wide + 1e-06)
        return first, scale

    def masks(k):
        last = days_ref[k]
        base = last - (DEPTH - 1)
        per_block = []
        for blk in range(128 // 16):
            s = slot + 16 * blk
            keep = indicator((s > last - w) & (s + DEPTH > last))if blk == 0 else indicator(s > last - w)
            if 16 * blk <= extra + FOLD - 1:
                n = s - base
                hi = indicator(fold & ((n == 0) | (n == 1) | (n == 4)))
                mid = indicator(fold & ((n == 2) | (n == 3)))
                low = indicator(fold & (n == 5))
                other = indicator(fold & ((n == 0) | (n == 2) | (n == 5)))
                other_mid = indicator(fold & ((n == 1) | (n == 3)))
                other_low = indicator(fold & (n == 4))
                per_block.append((keep, (hi, mid, low), (other, other_mid, other_low)))
            else:
                per_block.append((keep, None, None))
        late = indicator(slot + DEPTH <= last)
        return per_block, late

    def head_of(k, x, value, side):
        width = x.shape[1]
        per_block, late = masks(k)
        parts = [jnp.broadcast_to(p[k:k + 1], (16, width)).astype(BF) for p in value]
        blocks = []
        for blk, mk in enumerate(per_block):
            v = x[16 * blk:16 * blk + 16] * wide_mask(mk[0], width)
            if blk == 0:
                v = v + x[DEPTH:] * wide_mask(late, width)
            if mk[1] is not None:
                for p, m in zip(parts, mk[1 + side]):
                    v = v + p * wide_mask(m, width)
            blocks.append(v)
        return jnp.concatenate(blocks, axis=0)

    for c0 in range(0, N, chunk):
        at = pl.ds(c0, chunk)
        x = col_ref[:, at]
        first, scale = stats(x)
        a = scale * recip
        m = first * recip * a
        parts = split3(first)
        for k in range(K):
            col_a[k, :, at] = a[k:k + 1]
            col_m[k, :, at] = m[k:k + 1]
            col_head[k, :, at] = head_of(k, x, parts, 1)

    for c0 in range(0, M, chunk):
        at = pl.ds(c0, chunk)
        x = row_ref[:, at]
        first, scale = stats(x)
        both = jnp.concatenate([scale[:8], (first * scale)[:8]], axis=0)
        pad = jnp.concatenate([both, jnp.zeros((112, chunk), F32)], axis=0)
        row_stat[at, :] = pad.T
        parts = split3(-first * recip)
        for k in range(K):
            row_head[k, at, :] = head_of(k, x, parts, 0).T
        row_rest[at, :] = x[128:DEPTH].T

    step = 256 if N % 256 == 0 else 128
    G = M // tile

    def copy_out(i, k):
        b = lax.rem(i, 2)
        return pltpu.make_async_copy(obuf.at[b, k], out_ref.at[k, pl.ds(pl.multiple_of(i * tile, tile), tile), :],
                                     sems.at[b, k])

    def run(folded):
        def body(i, carry):
            b = lax.rem(i, 2)

            @pl.when(i >= 2)
            def _():
                for k in range(K):
                    copy_out(i - 2, k).wait()
            at = pl.ds(pl.multiple_of(i * tile, tile), tile)
            for k in range(K):
                lhs = jnp.concatenate([row_head[k, at, :], row_rest[at, :]], axis=1)
                s = jnp.broadcast_to(row_stat[at, k:k + 1], (tile, 128))
                s = jnp.concatenate([s] * (step // 128), axis=1)
                if not folded:
                    m = jnp.broadcast_to(row_stat[at, 8 + k:9 + k], (tile, 128))
                    m = jnp.concatenate([m] * (step // 128), axis=1)
                for j in range(0, N, step):
                    rhs = jnp.concatenate([col_head[k, :, j:j + step], col_ref[128:DEPTH, j:j + step]], axis=0)
                    g = jnp.dot(lhs, rhs, preferred_element_type=F32)
                    o = (g * s) * col_a[k, :, j:j + step]
                    if not folded:
                        o = o - m * col_m[k, :, j:j + step]
                    obuf[b, k, :, j:j + step] = o.astype(BF)
                copy_out(i, k).start()
            return carry

        lax.fori_loop(0, G, body, 0)

    @pl.when(fold)
    def _():
        run(True)

    @pl.when(jnp.logical_not(fold))
    def _():
        run(False)

    for i in range(max(0, G - 2), G):
        for k in range(K):
            copy_out(i, k).wait()


def correlate(window, out_days, rows, cols, tile=512, chunk=512):
    days, M = rows.shape
    N = cols.shape[1]
    K = out_days.shape[0]
    tile = min(tile, M)
    chunk = min(chunk, N, M)
    smem = pl.BlockSpec(memory_space=pltpu.SMEM)
    vmem = pl.BlockSpec(memory_space=pltpu.VMEM)
    return pl.pallas_call(
        functools.partial(corr_kernel, tile, chunk),
        out_shape=jax.ShapeDtypeStruct((K, M, N), BF),
        in_specs=[smem, smem, vmem, vmem],
        out_specs=pl.BlockSpec(memory_space=pl.ANY),
        scratch_shapes=[
            pltpu.VMEM((K, M, 128), BF),
            pltpu.VMEM((M, 128), BF),
            pltpu.VMEM((K, 128, N), BF),
            pltpu.VMEM((K, 1, N), F32),
            pltpu.VMEM((K, 1, N), F32),
            pltpu.VMEM((M, 128), F32),
            pltpu.VMEM((2, K, tile, N), BF),
            pltpu.SemaphoreType.DMA((2, K)),
        ],
        compiler_params=pltpu.CompilerParams(vmem_limit_bytes=60 * 2**20),
    )(window, out_days, rows, cols)


def on_device(returns, window, out_days):
    T, R, C = lax.axis_size("tm"), lax.axis_size("row"), lax.axis_size("col")
    rows, cols = gather(returns, T, R, C)
    return correlate(window, out_days, rows, cols)


def solution(mesh):
    return jax.shard_map(
        on_device,
        mesh=mesh,
        in_specs=(P("tm", ("row", "col")), P(), P()),
        out_specs=P(None, "row", ("col", "tm")),
        check_vma=False,
    )
```

time: 79.5 us -> 59.2 us (0.74)
  Pallas kernels: 78.7 us -> 58 us
    pallas_call x2, Pallas kernels: 78.7 us -> 58 us  [the longest x1 30.1 us: gather(): pl.pallas_call(functools.partial(gather_kernel, T, R, C, S), out_shape=(j...]
where the time goes in v1:
time: 59.2 us; the launch traced here: 58.7 us
  Pallas kernels  58 us (98%)
  between operations  0.66 us (1%)
    pallas_call x1, Pallas kernels, gather(): pl.pallas_call(functools.partial(gather_kernel, T, R, C, S), out_shape=(j...  30.1 us
    pallas_call x1, Pallas kernels, correlate(): pl.pallas_call(functools.partial(corr_kernel, tile, chunk), out_shape=jax...  27.9 us

profile of v1, /device:TPU:0, one launch (start us, length us, event | category | flops | bytes accessed | tf_op | source)
XLA Modules:
  0.0 58.7 jit_solution(7866739914814199499)
XLA Ops:
  0.7 30.1 %shard_map.37 = (bf16[272,4096]{1,0:T(8,128)(2,1)}, bf16[272,2048]{1,0:T(8,128)(2,1)}) custom-call(bf16[136,1024]{1,0:T(8,128)(2,1)} %x_ref.1), custom_call_target="tpu_custom_call" | custom-call | tf_op jit(solution)/shard_map/pallas_call | solution.py:207
  30.8 27.9 %shard_map.38 = bf16[4,4096,2048]{2,1,0:T(8,128)(2,1)} custom-call(s32[1]{0:T(128)S(6)} %copy.4.window_ref, s32[4]{0:T(128)} %days_ref.1, bf16[272,4096]{1,0:T(8,128)(2,1)} %get-tuple-element.7.row_ref, bf16[272,2048]{1,0:T(8,128)(2,1)} %get-tuple-element.8.col_ref), custom_call_target="tpu_custom_call" | custom-call | tf_op jit(solution)/shard_map/pallas_call | solution.py:393

commit v2 on v1

--- a/solution.py
+++ b/solution.py
@@ -242,16 +242,22 @@
     return jnp.concatenate([m] * (width // 128), axis=1)
 
 
-def corr_kernel(tile, chunk, window_ref, days_ref, row_ref, col_ref, out_ref,
-                row_head, row_rest, col_head, col_a, col_m, row_stat, obuf, sems):
+def corr_kernel(tile, chunk, window_ref, days_ref, rows_hbm, cols_hbm, out_ref,
+                row_ref, col_ref, mask_ref, head_a, rest_a, head_b, rest_b,
+                row_stat, row_p, col_head, col_a, col_m, obuf, sems, load_sems):
     K = days_ref.shape[0]
     days, M = row_ref.shape
     N = col_ref.shape[1]
     extra = days - DEPTH
+    heads = 128 // 16
     w = window_ref[0]
     wide = w.astype(F32)
     recip = 1.0 / wide
     fold = w <= DEPTH - FOLD
+    load_cols = pltpu.make_async_copy(cols_hbm, col_ref, load_sems.at[0])
+    load_rows = pltpu.make_async_copy(rows_hbm, row_ref, load_sems.at[1])
+    load_cols.start()
+    load_rows.start()
 
     kk = lax.broadcasted_iota(jnp.int32, (16, days), 0)
     day = lax.broadcasted_iota(jnp.int32, (16, days), 1)
@@ -261,6 +267,23 @@
     inside = indicator((day <= lasts) & (day > lasts - w))
 
     slot = lax.broadcasted_iota(jnp.int32, (16, 128), 0)
+    folded_blocks = (extra + FOLD - 1) // 16 + 1
+
+    for k in range(K):
+        last = days_ref[k]
+        for blk in range(heads):
+            s = slot + 16 * blk
+            keep = s > last - w
+            if blk == 0:
+                keep = keep & (s + DEPTH > last)
+            mask_ref[k, blk] = indicator(keep)
+        mask_ref[k, heads] = indicator(slot + DEPTH <= last)
+        for blk in range(folded_blocks):
+            n = slot + 16 * blk - (last - (DEPTH - 1))
+            sets = ((0, 1, 4), (2, 3), (5,), (0, 2, 5), (1, 3), (4,))
+            for e, members in enumerate(sets):
+                hit = functools.reduce(jnp.logical_or, [n == v for v in members])
+                mask_ref[k, heads + 1 + 6 * blk + e] = indicator(fold & hit)
 
     def stats(x):
         xf = x.astype(F32)
@@ -273,42 +296,21 @@
         scale = lax.rsqrt((second - first * first / wide) / wide + 1e-06)
         return first, scale
 
-    def masks(k):
-        last = days_ref[k]
-        base = last - (DEPTH - 1)
-        per_block = []
-        for blk in range(128 // 16):
-            s = slot + 16 * blk
-            keep = indicator((s > last - w) & (s + DEPTH > last))if blk == 0 else indicator(s > last - w)
-            if 16 * blk <= extra + FOLD - 1:
-                n = s - base
-                hi = indicator(fold & ((n == 0) | (n == 1) | (n == 4)))
-                mid = indicator(fold & ((n == 2) | (n == 3)))
-                low = indicator(fold & (n == 5))
-                other = indicator(fold & ((n == 0) | (n == 2) | (n == 5)))
-                other_mid = indicator(fold & ((n == 1) | (n == 3)))
-                other_low = indicator(fold & (n == 4))
-                per_block.append((keep, (hi, mid, low), (other, other_mid, other_low)))
-            else:
-                per_block.append((keep, None, None))
-        late = indicator(slot + DEPTH <= last)
-        return per_block, late
-
     def head_of(k, x, value, side):
         width = x.shape[1]
-        per_block, late = masks(k)
         parts = [jnp.broadcast_to(p[k:k + 1], (16, width)).astype(BF) for p in value]
         blocks = []
-        for blk, mk in enumerate(per_block):
-            v = x[16 * blk:16 * blk + 16] * wide_mask(mk[0], width)
+        for blk in range(heads):
+            v = x[16 * blk:16 * blk + 16] * wide_mask(mask_ref[k, blk], width)
             if blk == 0:
-                v = v + x[DEPTH:] * wide_mask(late, width)
-            if mk[1] is not None:
-                for p, m in zip(parts, mk[1 + side]):
-                    v = v + p * wide_mask(m, width)
+                v = v + x[DEPTH:] * wide_mask(mask_ref[k, heads], width)
+            if blk < folded_blocks:
+                for e, p in enumerate(parts):
+                    v = v + p * wide_mask(mask_ref[k, heads + 1 + 6 * blk + 3 * side + e], width)
             blocks.append(v)
         return jnp.concatenate(blocks, axis=0)
 
+    load_cols.wait()
     for c0 in range(0, N, chunk):
         at = pl.ds(c0, chunk)
         x = col_ref[:, at]
@@ -320,54 +322,80 @@
             col_a[k, :, at] = a[k:k + 1]
             col_m[k, :, at] = m[k:k + 1]
             col_head[k, :, at] = head_of(k, x, parts, 1)
+    load_rows.wait()
 
     for c0 in range(0, M, chunk):
         at = pl.ds(c0, chunk)
+        first, scale = stats(row_ref[:, at])
+        row_p[:, at] = (-first * recip)[:8]
+        both = jnp.concatenate([scale[:8], (first * scale)[:8]], axis=0)
+        row_stat[at, :] = jnp.concatenate([both, jnp.zeros((112, chunk), F32)], axis=0).T
+
+    def prepare(i, refs):
+        head, rest = refs
+        at = pl.ds(pl.multiple_of(i * tile, tile), tile)
         x = row_ref[:, at]
-        first, scale = stats(x)
-        both = jnp.concatenate([scale[:8], (first * scale)[:8]], axis=0)
-        pad = jnp.concatenate([both, jnp.zeros((112, chunk), F32)], axis=0)
-        row_stat[at, :] = pad.T
-        parts = split3(-first * recip)
+        parts = split3(row_p[:, at])
         for k in range(K):
-            row_head[k, at, :] = head_of(k, x, parts, 0).T
-        row_rest[at, :] = x[128:DEPTH].T
+            head[k] = head_of(k, x, parts, 0).T
+            if k == K - 1:
+                rest[...] = x[128:DEPTH].T
+            yield
 
     step = 256 if N % 256 == 0 else 128
     G = M // tile
 
-    def copy_out(i, k):
-        b = lax.rem(i, 2)
-        return pltpu.make_async_copy(obuf.at[b, k], out_ref.at[k, pl.ds(pl.multiple_of(i * tile, tile), tile), :],
-                                     sems.at[b, k])
+    span = N // 2 if N % (2 * step) == 0 else N
+    pieces = range(N // span)
+
+    def copy_out(i, b, k, h):
+        at = pl.ds(h * span, span)
+        return pltpu.make_async_copy(obuf.at[b, k, :, at],
+                                     out_ref.at[k, pl.ds(pl.multiple_of(i * tile, tile), tile), at],
+                                     sems.at[b, k, h])
+
+    def multiply(i, b, refs, folded, stages):
+        head, rest = refs
+        at = pl.ds(pl.multiple_of(i * tile, tile), tile)
+        for k in range(K):
+            lhs = jnp.concatenate([head[k], rest[...]], axis=1)
+            s = jnp.broadcast_to(row_stat[at, k:k + 1], (tile, 128))
+            s = jnp.concatenate([s] * (step // 128), axis=1)
+            if not folded:
+                m = jnp.broadcast_to(row_stat[at, 8 + k:9 + k], (tile, 128))
+                m = jnp.concatenate([m] * (step // 128), axis=1)
+            for j in range(0, N, step):
+                rhs = jnp.concatenate([col_head[k, :, j:j + step], col_ref[128:DEPTH, j:j + step]], axis=0)
+                g = jnp.dot(lhs, rhs, preferred_element_type=F32)
+                o = (g * s) * col_a[k, :, j:j + step]
+                if not folded:
+                    o = o - m * col_m[k, :, j:j + step]
+                obuf[b, k, :, j:j + step] = o.astype(BF)
+                if (j + step) % span == 0:
+                    copy_out(i, b, k, j // span).start()
+            next(stages, None)
+        for _ in stages:
+            pass
+
+    first_refs = (head_a, rest_a)
+    second_refs = (head_b, rest_b)
+    for _ in prepare(0, first_refs):
+        pass
 
     def run(folded):
-        def body(i, carry):
-            b = lax.rem(i, 2)
-
-            @pl.when(i >= 2)
-            def _():
-                for k in range(K):
-                    copy_out(i - 2, k).wait()
-            at = pl.ds(pl.multiple_of(i * tile, tile), tile)
-            for k in range(K):
-                lhs = jnp.concatenate([row_head[k, at, :], row_rest[at, :]], axis=1)
-                s = jnp.broadcast_to(row_stat[at, k:k + 1], (tile, 128))
-                s = jnp.concatenate([s] * (step // 128), axis=1)
-                if not folded:
-                    m = jnp.broadcast_to(row_stat[at, 8 + k:9 + k], (tile, 128))
-                    m = jnp.concatenate([m] * (step // 128), axis=1)
-                for j in range(0, N, step):
-                    rhs = jnp.concatenate([col_head[k, :, j:j + step], col_ref[128:DEPTH, j:j + step]], axis=0)
-                    g = jnp.dot(lhs, rhs, preferred_element_type=F32)
-                    o = (g * s) * col_a[k, :, j:j + step]
-                    if not folded:
-                        o = o - m * col_m[k, :, j:j + step]
-                    obuf[b, k, :, j:j + step] = o.astype(BF)
-                copy_out(i, k).start()
+        def body(p, carry):
+            for b, (now, later) in enumerate(((first_refs, second_refs), (second_refs, first_refs))):
+                i = 2 * p + b
+
+                @pl.when(p > 0)
+                def _():
+                    for k in range(K):
+                        for h in pieces:
+                            copy_out(i - 2, b, k, h).wait()
+                multiply(i, b, now, folded, prepare(jnp.minimum(i + 1, G - 1), later))
             return carry
 
-        lax.fori_loop(0, G, body, 0)
+        lax.fori_loop(0, G // 2, body, 0)
 
     @pl.when(fold)
     def _():
@@ -377,33 +405,40 @@
     def _():
         run(False)
 
-    for i in range(max(0, G - 2), G):
+    for b in range(2):
         for k in range(K):
-            copy_out(i, k).wait()
+            for h in pieces:
+                copy_out(G - 2 + b, b, k, h).wait()
 
 
 def correlate(window, out_days, rows, cols, tile=512, chunk=512):
     days, M = rows.shape
     N = cols.shape[1]
     K = out_days.shape[0]
-    tile = min(tile, M)
+    tile = min(tile, M // 2)
     chunk = min(chunk, N, M)
+    folded_blocks = (days - DEPTH + FOLD - 1) // 16 + 1
     smem = pl.BlockSpec(memory_space=pltpu.SMEM)
-    vmem = pl.BlockSpec(memory_space=pltpu.VMEM)
+    hbm = pl.BlockSpec(memory_space=pl.ANY)
+    side = [pltpu.VMEM((K, tile, 128), BF), pltpu.VMEM((tile, 128), BF)]
     return pl.pallas_call(
         functools.partial(corr_kernel, tile, chunk),
         out_shape=jax.ShapeDtypeStruct((K, M, N), BF),
-        in_specs=[smem, smem, vmem, vmem],
-        out_specs=pl.BlockSpec(memory_space=pl.ANY),
+        in_specs=[smem, smem, hbm, hbm],
+        out_specs=hbm,
         scratch_shapes=[
-            pltpu.VMEM((K, M, 128), BF),
-            pltpu.VMEM((M, 128), BF),
+            pltpu.VMEM((days, M), BF),
+            pltpu.VMEM((days, N), BF),
+            pltpu.VMEM((K, 9 + 6 * folded_blocks, 16, 128), BF),
+            *side, *side,
+            pltpu.VMEM((M, 128), F32),
+            pltpu.VMEM((8, M), F32),
             pltpu.VMEM((K, 128, N), BF),
             pltpu.VMEM((K, 1, N), F32),
             pltpu.VMEM((K, 1, N), F32),
-            pltpu.VMEM((M, 128), F32),
             pltpu.VMEM((2, K, tile, N), BF),
-            pltpu.SemaphoreType.DMA((2, K)),
+            pltpu.SemaphoreType.DMA((2, K, 2)),
+            pltpu.SemaphoreType.DMA((2,)),
         ],
         compiler_params=pltpu.CompilerParams(vmem_limit_bytes=60 * 2**20),
     )(window, out_days, rows, cols)

time: 59.2 us -> 57.6 us (0.973)
  Pallas kernels: 58 us -> 56.2 us
    pallas_call x1, Pallas kernels: 27.9 us -> 26.1 us  [correlate(): pl.pallas_call(functools.partial(corr_kernel, tile, chunk), out_shape=jax...]
where the time goes in v2:
time: 57.6 us; the launch traced here: 57.1 us
  Pallas kernels  56.2 us (98%)
  between operations  0.82 us (1%)
    pallas_call x1, Pallas kernels, gather(): pl.pallas_call(functools.partial(gather_kernel, T, R, C, S), out_shape=(j...  30.1 us
    pallas_call x1, Pallas kernels, correlate(): pl.pallas_call(functools.partial(corr_kernel, tile, chunk), out_shape=jax...  26.1 us

profile of v2, /device:TPU:0, one launch (start us, length us, event | category | flops | bytes accessed | tf_op | source)
XLA Modules:
  0.0 57.1 jit_solution(2290003385741951540)
XLA Ops:
  0.7 30.1 %shard_map.37 = (bf16[272,4096]{1,0:T(8,128)(2,1)}, bf16[272,2048]{1,0:T(8,128)(2,1)}) custom-call(bf16[136,1024]{1,0:T(8,128)(2,1)} %x_ref.1), custom_call_target="tpu_custom_call" | custom-call | tf_op jit(solution)/shard_map/pallas_call | solution.py:207
  30.8 26.1 %shard_map.38 = bf16[4,4096,2048]{2,1,0:T(8,128)(2,1)} custom-call(s32[1]{0:T(128)S(6)} %copy.4.window_ref, s32[4]{0:T(128)} %days_ref.1, bf16[272,4096]{1,0:T(8,128)(2,1)} %get-tuple-element.7.rows_hbm, bf16[272,2048]{1,0:T(8,128)(2,1)} %get-tuple-element.8.cols_hbm), custom_call_target="tpu_custom_call" | custom-call | tf_op jit(solution)/shard_map/pallas_call | solution.py:424

commit v3 on v2

--- a/solution.py
+++ b/solution.py
@@ -411,7 +411,7 @@
                 copy_out(G - 2 + b, b, k, h).wait()
 
 
-def correlate(window, out_days, rows, cols, tile=512, chunk=512):
+def correlate(window, out_days, rows, cols, tile=512, chunk=1024):
     days, M = rows.shape
     N = cols.shape[1]
     K = out_days.shape[0]

time: 57.6 us -> 57.8 us (level)
  no operation moved by 1% of the time
where the time goes in v3:
time: 57.8 us; the launch traced here: 57.3 us
  Pallas kernels  56.5 us (98%)
  between operations  0.82 us (1%)
    pallas_call x1, Pallas kernels, gather(): pl.pallas_call(functools.partial(gather_kernel, T, R, C, S), out_shape=(j...  30.1 us
    pallas_call x1, Pallas kernels, correlate(): pl.pallas_call(functools.partial(corr_kernel, tile, chunk), out_shape=jax...  26.3 us

profile of v3, /device:TPU:0, one launch (start us, length us, event | category | flops | bytes accessed | tf_op | source)
XLA Modules:
  0.0 57.3 jit_solution(2508726333660848532)
XLA Ops:
  0.7 30.1 %shard_map.37 = (bf16[272,4096]{1,0:T(8,128)(2,1)}, bf16[272,2048]{1,0:T(8,128)(2,1)}) custom-call(bf16[136,1024]{1,0:T(8,128)(2,1)} %x_ref.1), custom_call_target="tpu_custom_call" | custom-call | tf_op jit(solution)/shard_map/pallas_call | solution.py:207
  30.8 26.3 %shard_map.38 = bf16[4,4096,2048]{2,1,0:T(8,128)(2,1)} custom-call(s32[1]{0:T(128)S(6)} %copy.4.window_ref, s32[4]{0:T(128)} %days_ref.1, bf16[272,4096]{1,0:T(8,128)(2,1)} %get-tuple-element.7.rows_hbm, bf16[272,2048]{1,0:T(8,128)(2,1)} %get-tuple-element.8.cols_hbm), custom_call_target="tpu_custom_call" | custom-call | tf_op jit(solution)/shard_map/pallas_call | solution.py:424
